TPU v7x, 32 devices: a whole 2x2x4 slice. The times are simulated.
32 devices in a mesh: row: 8 (over z, y), col: 4 (over x, core).
Axes of the slice: x: 2, y: 2, z: 4, core: 2. Of those that a mesh axis runs over, the one named last changes fastest.
Arguments:
- spectra: bfloat16 [1024, 16, 128], P(('row', 'col')), may hold values from -4 to 4
- window_flags: int32 [1024, 64], P(('row', 'col')), may hold values 0 or 1
- pair_mask: int32 [1024, 1024], P('row', 'col'), may hold values 0 or 1
- misfit_weight: bfloat16 [16, 1024, 1024], P(None, 'row', 'col'), may hold values from 0.0099487305 to 0.099609375
- observed: bfloat16 [2, 16, 1024, 1024], P(None, None, 'row', 'col'), may hold values from -6 to 6
Outputs:
- grad_first: bfloat16 [1024, 16, 128], P(('row', 'col'))
- grad_second: bfloat16 [4, 256, 16, 128], P('col', 'row')
All inputs are finite; a program needn't handle non-finite values. No bound on the sum of `window_flags` or of `pair_mask` on one device may be relied on, other than what follows from the above.
Results may differ from a plain program's by a relative error of at most 0.019.
Values may be sent and summed in bfloat16 or wider, within the bound.
No kernel may reach another device: no remote copies, remote signals or barrier semaphores. Data moves between devices by JAX's collectives and lax.ppermute only.
A program may use at most 64 MiB of HBM per device.

v0:
```python
import jax
import jax.numpy as jnp
from jax import lax
from jax.sharding import PartitionSpec as P


def swap_parts(values, half_width):
    return jnp.concatenate([-values[..., half_width:], values[..., :half_width]], axis=-1)


def per_device(spectra, window_flags, pair_mask, misfit_weight, observed):
    half_width = spectra.shape[2] // 2
    flag_value = window_flags.astype(jnp.bfloat16)
    flag_both = jnp.concatenate([flag_value, flag_value], axis=1)
    flagged = spectra * flag_both[:, None, :]
    first_side = lax.all_gather(flagged, "col", axis=0, tiled=True)
    block_ratio = lax.axis_size("row") // lax.axis_size("col")
    strided = lax.all_gather(flagged, "row", axis=0, tiled=True)
    regrouped = lax.all_to_all(strided, "col", split_axis=0, concat_axis=0, tiled=True)
    col_count = lax.axis_size("col")
    shard_rows = flagged.shape[0]
    regrouped = regrouped.reshape(
        col_count, block_ratio, shard_rows, flagged.shape[1], flagged.shape[2]
    )
    second_side = jnp.transpose(regrouped, (1, 0, 2, 3, 4)).reshape(
        -1, flagged.shape[1], flagged.shape[2]
    )
    col_stack = jnp.stack([second_side, swap_parts(second_side, half_width)])
    row_stack = jnp.stack([first_side, -swap_parts(first_side, half_width)])
    cross_spec = jnp.einsum(
        "ifk,cjfk->cfij", first_side, col_stack, preferred_element_type=jnp.float32
    )
    residual = (
        pair_mask.astype(jnp.float32)[None, None]
        * misfit_weight.astype(jnp.float32)[None]
        * (cross_spec - observed.astype(jnp.float32))
    ).astype(jnp.bfloat16)
    residual_part = residual
    grad_first = lax.psum_scatter(
        jnp.einsum(
            "cfij,cjfk->ifk", residual_part, col_stack, preferred_element_type=jnp.float32
        ).astype(jnp.bfloat16),
        "col",
        scatter_dimension=0,
        tiled=True,
    )
    residual_part = residual
    grad_second = lax.psum_scatter(
        jnp.einsum(
            "cfij,cifk->jfk", residual_part, row_stack, preferred_element_type=jnp.float32
        ).astype(jnp.bfloat16),
        "row",
        scatter_dimension=0,
        tiled=True,
    )
    return (grad_first, grad_second[None])


def solution(mesh):
    placed = (
        P(("row", "col"), None, None),
        P(("row", "col"), None),
        P("row", "col"),
        P(None, "row", "col"),
        P(None, None, "row", "col"),
    )
    return jax.shard_map(
        per_device,
        mesh=mesh,
        in_specs=placed,
        out_specs=(P(("row", "col"), None, None), P("col", "row", None, None)),
        check_vma=False,
    )
```

profile of v0, /device:TPU:0, one launch (start us, length us, event | category | flops | bytes accessed | tf_op | source)
XLA Modules:
  0.0 180.4 jit_solution(5672547921688887537)
XLA Ops:
  7.2 0.0 all-gather.2.cloned.1.call-start
  7.2 0.7 convert_element_type.27
  7.9 0.1 pad_maximum_fusion.7
  8.0 1.6 copy_multiply_fusion
  9.6 0.0 all-gather.2.cloned.1.call-update
  9.6 43.1 %all-gather.2.cloned.1.call-done = bf16[256,16,128]{2,0,1:T(8,128)(2,1)} async-done(((bf16[32,16,128]{2,0,1:T(8,128)(2,1)}), bf16[256,16,128]{2,0,1:T(8,128)(2,1)}) %all-gather.2.cloned.1.call-update) | async-done | bytes 1048592 | tf_op jit(solution)/shard_map/all_gather | solution.py:18
  52.7 2.9 %copy.19 = bf16[256,16,128]{2,1,0:T(8,128)(2,1)} copy(bf16[256,16,128]{2,0,1:T(8,128)(2,1)} %all-gather.2.cloned.1.call-done) | data formatting | bytes 2097152 | tf_op jit(solution)/shard_map/all_gather | solution.py:18
  55.6 4.2 %all-to-all-start = ((bf16[256,16,128]{2,1,0:T(8,128)(2,1)}), bf16[256,16,128]{2,1,0:T(8,128)(2,1)}, u32[]{:S(2)}, u32[]{:S(2)}) async-start(bf16[256,16,128]{2,1,0:T(8,128)(2,1)} %copy.19), calls=%async_computation | async-start | bytes 2097152 | tf_op jit(solution)/shard_map/all_to_all | solution.py:19
  59.9 0.0 reduce-scatter.3.cloned.1.call-start
  60.0 1.6 convert_multiply_fusion
  61.5 1.9 %copy.21 = f32[16,128,256]{1,2,0:T(8,128)S(1)} copy(f32[16,128,256]{2,1,0:T(8,128)} %convert_multiply_fusion) | data formatting | bytes 4194304 | tf_op jit(solution)/shard_map/mul | solution.py:34
  63.4 0.0 copy-start.3
  63.4 4.0 %copy.22 = bf16[2,16,128,256]{2,3,0,1:T(8,128)(2,1)} copy(bf16[2,16,128,256]{3,2,1,0:T(8,128)(2,1)} %param.9) | data formatting | bytes 4194304 | tf_op args[4]
  67.4 10.5 %all_gather.7 = bf16[128,16,128]{2,0,1:T(8,128)(2,1)S(1)} all-gather(bf16[32,16,128]{2,0,1:T(8,128)(2,1)S(1)} %copy-done.3), channel_id=1, replica_groups=mesh['row'=8,'col'=4] {'col'}, dimensions={0}, use_global_device_ids=true | all-gather | bytes 655360 | tf_op jit(solution)/shard_map/all_gather | solution.py:16
  77.9 1.5 copy.20
  79.4 0.4 slice_negate_fusion
  79.9 0.6 maximum_bitcast_fusion
  80.5 1.0 copy-done
  81.5 0.9 fusion.1
  82.4 1.3 copy-done.1
  83.7 0.8 fusion.10
  84.5 1.2 copy.25
  85.7 0.0 reduce-scatter.3.cloned.1.call-update
  85.8 0.0 reduce-scatter.5.cloned.1.call-start
  85.8 0.2 fusion.14
  86.0 0.3 maximum_negate_fusion
  86.4 0.9 copy-done.2
  87.3 1.9 %fusion.6 = bf16[256,16,128]{0,2,1:T(8,128)(2,1)} fusion(bf16[2,16,128,256]{2,3,0,1:T(8,128)(2,1)S(1)} %copy-done.2, bf16[1,128,16,128]{3,1,2,0:T(8,128)(2,1)S(1)} %maximum_negate_fusion, bf16[1,128,16,128]{3,1,2,0:T(8,128)(2,1)S(1)} %bitcast.44), kind=kOutput, calls=%fused_computation.8 | convolution fusion | flops 269484032 | bytes 4194304 | tf_op jit(solution)/shard_map/cfij,cifk->jfk/dot_general | solution.py:49
  89.2 2.6 %copy.28 = bf16[256,16,128]{2,1,0:T(8,128)(2,1)} copy(bf16[256,16,128]{0,2,1:T(8,128)(2,1)} %fusion.6) | data formatting | bytes 2097152 | tf_op jit(solution)/shard_map/convert_element_type | solution.py:51
  91.8 0.0 reduce-scatter.5.cloned.1.call-update
  91.8 13.8 %reduce-scatter.3.cloned.1.call-done = bf16[32,16,128]{2,1,0:T(8,128)(2,1)} async-done(((bf16[128,16,128]{2,1,0:T(8,128)(2,1)}), bf16[32,16,128]{2,1,0:T(8,128)(2,1)}) %reduce-scatter.3.cloned.1.call-update) | async-done | bytes 131088 | tf_op jit(solution)/shard_map/reduce_scatter | solution.py:39
  105.7 68.2 %reduce-scatter.5.cloned.1.call-done = bf16[32,16,128]{2,1,0:T(8,128)(2,1)} async-done(((bf16[256,16,128]{2,1,0:T(8,128)(2,1)}), bf16[32,16,128]{2,1,0:T(8,128)(2,1)}) %reduce-scatter.5.cloned.1.call-update) | async-done | bytes 131088 | tf_op jit(solution)/shard_map/reduce_scatter | solution.py:48
  (10 shorter events, 0.0 us)
Async XLA Ops:
  7.2 45.6 %all-gather.2.cloned.1.call-start = ((), (), s32[]{:S(2)}) async-start(), calls=%async_computation.3 | async-start | bytes 1179648 | tf_op jit(solution)/shard_map/all_gather | solution.py:18
  9.6 50.3 %copy-start.5 = (s32[128,256]{1,0:T(8,128)S(1)}, s32[128,256]{1,0:T(8,128)}, u32[]{:S(2)}) copy-start(s32[128,256]{1,0:T(8,128)} %param.7) | copy-start | bytes 393220
  9.6 50.3 %copy-start.4 = (bf16[16,128,256]{2,1,0:T(8,128)(2,1)S(1)}, bf16[16,128,256]{2,1,0:T(8,128)(2,1)}, u32[]{:S(2)}) copy-start(bf16[16,128,256]{2,1,0:T(8,128)(2,1)} %param.8) | copy-start | bytes 3145732
  55.6 22.3 %all-to-all-start = ((bf16[256,16,128]{2,1,0:T(8,128)(2,1)}), bf16[256,16,128]{2,1,0:T(8,128)(2,1)}, u32[]{:S(2)}, u32[]{:S(2)}) async-start(bf16[256,16,128]{2,1,0:T(8,128)(2,1)} %copy.19), calls=%async_computation | async-start | bytes 2097152 | tf_op jit(solution)/shard_map/all_to_all | solution.py:19
  59.9 45.8 %reduce-scatter.3.cloned.1.call-start = ((), (), s32[]{:S(2)}) async-start(), calls=%async_computation.4 | async-start | bytes 655360 | tf_op jit(solution)/shard_map/reduce_scatter | solution.py:39
  63.4 4.0 %copy-start.3 = (bf16[32,16,128]{2,0,1:T(8,128)(2,1)S(1)}, bf16[32,16,128]{2,0,1:T(8,128)(2,1)}, u32[]{:S(2)}) copy-start(bf16[32,16,128]{2,0,1:T(8,128)(2,1)} %copy_multiply_fusion) | copy-start | bytes 393220
  79.9 1.6 copy-start
  82.4 1.3 copy-start.1
  85.7 1.6 copy-start.2
  85.8 88.1 %reduce-scatter.5.cloned.1.call-start = ((), (), s32[]{:S(2)}) async-start(), calls=%async_computation.5 | async-start | bytes 1179648 | tf_op jit(solution)/shard_map/reduce_scatter | solution.py:48
Sparse Core Ops, SparseCore 0:
  10.6 42.1 all-gather.1
  85.9 19.7 reduce-scatter.2
  109.7 64.1 reduce-scatter.4
where the time goes:
time: 181 us; the launch traced here: 180 us
  waiting for transfers between devices  125 us (69%)
  local copies, waits for them, and re-layouts  17.4 us (10%)
  between operations  13.9 us (8%)
  blocking collectives  10.5 us (6%)
  other arithmetic  5.54 us (3%)
  starting transfers between devices  4.37 us (2%)
  matrix products  3.59 us (2%)
    reduce_scatter x1, waiting for transfers between devices, per_device(): lax.psum_scatter(jnp.einsum('cfij,cifk->jfk', residual_part, row_stack, p...  68.2 us
    all_gather x1, waiting for transfers between devices, per_device(): strided = lax.all_gather(flagged, 'row', axis=0, tiled=True)  43.1 us
    reduce_scatter x1, waiting for transfers between devices, per_device(): lax.psum_scatter(jnp.einsum('cfij,cjfk->ifk', residual_part, col_stack, p...  13.8 us
    all_gather x1, blocking collectives, per_device(): first_side = lax.all_gather(flagged, 'col', axis=0, tiled=True)  10.5 us
    unnamed x13, local copies, waits for them, and re-layouts  7.28 us
    all_to_all x1, starting transfers between devices, per_device(): lax.all_to_all(strided, 'col', split_axis=0, concat_axis=0, tiled=True)  4.24 us
  transfers between devices with their start and end apart: 4, of which 3 were waited for; matrix products, arithmetic and copies ran while one was open for 7% of the time, Pallas kernels for 0%

commit v1 on v0

v1 whole, which is shorter than its diff:
```python
import functools
import math

import jax
import jax.numpy as jnp
from jax import lax
from jax.experimental import pallas as pl
from jax.experimental.pallas import tpu as pltpu
from jax.sharding import PartitionSpec as P


AXES = ("row", "col")
F32 = jnp.float32
BF16 = jnp.bfloat16
SPARE = 2 << 20
WAIT_FLOPS = 5 * 10**9
UNROLL = 8
CUTS = (0, 8, 16)
PARTS = len(CUTS) - 1
GROUP = 2


def place(ratio):
    row = lax.axis_index("row")
    return row // ratio, row % ratio, lax.axis_index("col")


def spread(col, cols):
    return col // 2 + (col % 2) * (cols // 2)


def unspread(plane, cols):
    return (2 * plane) % cols + (2 * plane) // cols


def at(slot, n):
    return pl.ds(pl.multiple_of(slot * n, n), n)


def kernel_call(body, outs, scratch, flops, args):
    shapes = [jax.ShapeDtypeStruct(*o) for o in outs]
    moved = sum(a.size * a.dtype.itemsize for a in (*args, *shapes))
    held = sum(math.prod(m.shape) * jnp.dtype(m.dtype).itemsize for m in scratch)
    near = pl.BlockSpec(memory_space=pltpu.VMEM)
    return pl.pallas_call(
        body,
        out_shape=shapes,
        in_specs=[near] * len(args),
        out_specs=[near] * len(outs),
        scratch_shapes=scratch,
        compiler_params=pltpu.CompilerParams(vmem_limit_bytes=moved + held + SPARE),
        cost_estimate=pl.CostEstimate(
            flops=flops, bytes_accessed=moved, transcendentals=0
        ),
    )(*args)


def flag_body(spectra, flags, *refs):
    outs, wide = refs[:-1], refs[-1]
    n, freqs, width = spectra.shape
    half = flags.shape[1]
    copies = lax.broadcasted_iota(jnp.int32, (half, width), 1) % half
    copies = (copies == lax.broadcasted_iota(jnp.int32, (half, width), 0)).astype(BF16)
    both = jnp.dot(flags[...].astype(F32).astype(BF16), copies, preferred_element_type=F32)
    wide[...] = spectra[...].astype(F32).reshape(n * freqs, width)
    f = 0
    for out in outs:
        for i in range(out.shape[0]):
            out[i] = (wide[pl.ds(f, n, stride=freqs), :] * both).astype(BF16)
            f += 1


def join_body(ratio, own, mate, out):
    core = place(ratio)[2] % 2
    n = own.shape[1]
    out[:, at(core, n), :] = own[...]
    out[:, at(1 - core, n), :] = mate[...]


def turned(value, width):
    lane = lax.broadcasted_iota(jnp.int32, value.shape, 1)
    sign = jnp.where(lane < width // 2, 1.0, -1.0).astype(F32)
    return pltpu.roll(value.astype(F32), width // 2, 1) * sign


def side_stack(left, f):
    mine = left[f]
    return jnp.concatenate([mine, turned(mine, mine.shape[1]).astype(BF16)], axis=0)


def pair_body(cols, ratio, d, start, *refs):
    half = cols // 2
    side, rest = refs[:half], refs[half:]
    pieces, rest = rest[:half], rest[half:]
    (mask, weight, observed), rest = rest[:3], rest[3:]
    earlier, rest = rest[:d], rest[d:]
    residuals, outs, (left, right, second) = rest[0], rest[1:-3], rest[-3:]
    plane, turn, col = place(ratio)
    freqs, rows, _ = left.shape
    n = rows // cols
    for k in range(half):
        left[:, at((col // 2) ^ k, 2 * n), :] = side[k][...]
        right[:, at(unspread(plane ^ k, cols) // 2, 2 * n), :] = pieces[k][...]
    columns = at(turn ^ d, rows)
    last = d == ratio - 1

    def one(i, _):
        f = start + i
        stack = side_stack(left, i)
        cross = lax.dot_general(
            stack, right[i], (((1,), (1,)), ((), ())), preferred_element_type=F32
        )
        scale = mask[:, columns].astype(F32) * weight[f, :, columns].astype(F32)
        real = scale * (cross[:rows] - observed[0, f, :, columns].astype(F32))
        imag = scale * (cross[rows:] - observed[1, f, :, columns].astype(F32))
        residual = jnp.concatenate([real.astype(BF16), imag.astype(BF16)], axis=0)
        residuals[i] = residual
        sums = lax.dot_general(
            residual, stack, (((0,), (0,)), ((), ())), preferred_element_type=F32
        ).astype(BF16)
        if last:
            second[i, columns] = sums
        else:
            outs[0][i] = sums
        return 0

    lax.fori_loop(0, freqs, one, 0, unroll=min(UNROLL, freqs))
    if not last:
        return
    for e, block in enumerate(earlier):
        second[:, at(turn ^ e, rows), :] = block[...]
    kept, sent = outs[:cols], outs[cols:]
    for m in range(cols):
        slot = (plane ^ m) * ratio
        kept[m][...] = second[:, at(slot + turn, n), :]
        group, spot = divmod(m, GROUP)
        for e in range(1, ratio):
            there = second[:, at(slot + (turn ^ e), n), :]
            sent[group * (ratio - 1) + e - 1][:, spot * n : (spot + 1) * n, :] = there


def first_body(cols, ratio, parts, *refs):
    half = cols // 2
    per = ratio * (half + 1)
    groups, rest = [refs[q * per : (q + 1) * per] for q in range(parts)], refs[parts * per :]
    odd, evens, (right, first) = rest[0], rest[1:-2], rest[-2:]
    plane, _, col = place(ratio)
    _, rows, width = first.shape
    n = rows // cols
    start = 0
    for group in groups:
        pieces, residuals = group[: ratio * half], group[ratio * half :]
        size = residuals[0].shape[0]
        for d in range(ratio):
            for k in range(half):
                slot = d * half + unspread(plane ^ k, cols) // 2
                right[:size, at(slot, 2 * n), :] = pieces[d * half + k][...]

        def one(i, _, residuals=residuals, start=start):
            both = 0.0
            for d in range(ratio):
                other = right[i, d * rows : (d + 1) * rows]
                both += jnp.dot(residuals[d][i], other, preferred_element_type=F32)
            first[start + i] = (both[:rows] - turned(both[rows:], width)).astype(BF16)
            return 0

        lax.fori_loop(0, size, one, 0, unroll=min(UNROLL, size))
        start += size
    for k in range(half):
        evens[k][...] = first[:, at(col ^ (2 * k), n), :]
        odd[:, k * n : (k + 1) * n, :] = first[:, at(col ^ (2 * k + 1), n), :]


def fold_body(spots, *refs):
    terms, out = refs[:-1], refs[-1]
    n = out.shape[1]
    total = 0.0
    for spot, term in zip(spots, terms):
        total += term[:, spot * n : (spot + 1) * n, :].astype(F32)
    out[...] = total.astype(BF16)


def finish_body(spots, parts, *refs):
    out, wide = refs[-2:]
    n, freqs, width = out.shape
    f = 0
    for q in range(parts):
        terms = refs[q * len(spots) : (q + 1) * len(spots)]
        for i in range(terms[0].shape[0]):
            total = 0.0
            for spot, term in zip(spots, terms):
                total += term[i, spot * n : (spot + 1) * n].astype(F32)
            wide[pl.ds(f, n, stride=freqs), :] = total
            f += 1
    out[...] = wide[...].reshape(n, freqs, width).astype(BF16)


def per_device(row_count, cols, spectra, window_flags, pair_mask, misfit_weight, observed):
    ratio = row_count // cols
    half = cols // 2
    n, freqs, width = spectra.shape
    rows = cols * n
    bounds = [freqs * cut // CUTS[-1] for cut in CUTS]
    sizes = [b - a for a, b in zip(bounds, bounds[1:])]

    def send(value, where):
        pairs = []
        for row in range(row_count):
            for col in range(cols):
                plane, turn, to = where(row // ratio, row % ratio, col)
                pairs.append((row * cols + col, (plane * ratio + turn) * cols + to))
        return lax.ppermute(value, AXES, pairs)

    def piece(size, count=1):
        return ((size, count * n, width), BF16)

    owns = kernel_call(
        flag_body,
        [piece(size) for size in sizes],
        [pltpu.VMEM((n * freqs, width), F32)],
        WAIT_FLOPS,
        (spectra, window_flags),
    )
    first_args, second_args = [], []
    for q, (size, own) in enumerate(zip(sizes, owns)):
        mate = send(own, lambda z, t, c: (z, t, c ^ 1))
        (chip,) = kernel_call(
            functools.partial(join_body, ratio), [piece(size, 2)], [], own.size, (own, mate)
        )
        pieces = [send(chip, lambda z, t, c: (spread(c, cols) ^ k, t, z)) for k in range(half)]
        side = [chip] + [send(chip, lambda z, t, c: (z, t, c ^ (2 * k))) for k in range(1, half)]
        for d in range(1, ratio):
            for k in range(half):
                there = send(pieces[k], lambda z, t, c: (z, t ^ d, c))
                pieces.append(there)
        blocks, residuals = [], []
        groups = cols // GROUP
        for d in range(ratio):
            last = d == ratio - 1
            results = [piece(size)] * cols + [piece(size, GROUP)] * (groups * (ratio - 1))
            near = pieces[d * half : (d + 1) * half]
            found, *outs = kernel_call(
                functools.partial(pair_body, cols, ratio, d, bounds[q]),
                [((size, 2 * rows, rows), BF16)] + (results if last else [piece(size, cols)]),
                [
                    pltpu.VMEM((size, rows, width), BF16),
                    pltpu.VMEM((size, rows, width), BF16),
                    pltpu.VMEM((size, rows * ratio, width), BF16),
                ],
                8 * size * rows * rows * width,
                (*side, *near, pair_mask, misfit_weight, observed, *blocks),
            )
            residuals.append(found)
            blocks += outs
        first_args += [*pieces, *residuals]
        kept, sent = blocks[ratio - 1 :][:cols], blocks[ratio - 1 :][cols:]
        back = [[] for _ in range(groups)]
        for g in range(groups):
            for d in range(1, ratio):
                value = sent[g * (ratio - 1) + d - 1]
                there = send(value, lambda z, t, c: (z, t ^ d, c))
                back[g].append(there)
        second_args += [kept[0], *back[0]]
        for m in range(1, cols):
            spots = (0,) + (m % GROUP,) * (ratio - 1)
            (folded,) = kernel_call(
                functools.partial(fold_body, spots),
                [piece(size)],
                [],
                ratio * own.size,
                (kept[m], *back[m // GROUP]),
            )
            there = send(folded, lambda z, t, c: (z ^ m, t, c))
            second_args.append(there)

    odd, *evens = kernel_call(
        functools.partial(first_body, cols, ratio, PARTS),
        [piece(freqs, half)] + [piece(freqs)] * half,
        [
            pltpu.VMEM((max(sizes), rows * ratio, width), BF16),
            pltpu.VMEM((freqs, rows, width), BF16),
        ],
        4 * freqs * rows * rows * ratio * width,
        first_args,
    )
    odd = send(odd, lambda z, t, c: (z, t, c ^ 1))
    first_terms = [evens[0], odd]
    for k in range(1, half):
        (folded,) = kernel_call(
            functools.partial(fold_body, (0, k)), [piece(freqs)], [], n, (evens[k], odd)
        )
        there = send(folded, lambda z, t, c: (z, t, c ^ (2 * k)))
        first_terms.append(there)

    def finish(parts, terms):
        (out,) = kernel_call(
            functools.partial(finish_body, (0,) * (len(terms) // parts), parts),
            [((n, freqs, width), BF16)],
            [pltpu.VMEM((n * freqs, width), F32)],
            cols * spectra.size,
            terms,
        )
        return out

    grad_first = finish(1, first_terms)
    return grad_first, finish(PARTS, second_args)[None]


def solution(mesh):
    placed = (
        P(AXES, None, None),
        P(AXES, None),
        P("row", "col"),
        P(None, "row", "col"),
        P(None, None, "row", "col"),
    )
    row_count, cols = mesh.shape["row"], mesh.shape["col"]
    ratio = row_count // cols
    for count in (cols, ratio):
        assert count & (count - 1) == 0 and cols % GROUP == 0 and cols > 1, "mesh sizes"

    def body(*args):
        return per_device(row_count, cols, *args)

    return jax.shard_map(
        body,
        mesh=mesh,
        in_specs=placed,
        out_specs=(P(AXES, None, None), P("col", "row", None, None)),
        check_vma=False,
    )
```

time: 181 us -> 58.9 us (0.33)
  waiting for transfers between devices: 125 us -> 16.5 us
  starting transfers between devices: 4.37 us -> 33 us
  local copies, waits for them, and re-layouts: 17.4 us -> 1.78 us
  between operations: 13.9 us -> 0.79 us
  blocking collectives: 10.5 us -> 0 us
  Pallas kernels: 0 us -> 6.5 us
  other arithmetic: 5.54 us -> 0 us
  matrix products: 3.59 us -> 0 us
    reduce_scatter x2 -> x0, waiting for transfers between devices: 82.1 us -> none  [the longest x1 68.2 us: per_device(): lax.psum_scatter(jnp.einsum('cfij,cifk->jfk', residual_part, row_stack, p...]
    all_gather x1 -> x0, waiting for transfers between devices: 43.1 us -> none  [per_device(): strided = lax.all_gather(flagged, 'row', axis=0, tiled=True)]
    ppermute x0 -> x24, starting transfers between devices: none -> 33 us  [send(): return lax.ppermute(value, AXES, pairs)]
    ppermute x0 -> x24, waiting for transfers between devices: none -> 16.5 us  [send(): return lax.ppermute(value, AXES, pairs)]
    all_gather x1 -> x0, blocking collectives: 10.5 us -> none  [per_device(): first_side = lax.all_gather(flagged, 'col', axis=0, tiled=True)]
    pallas_call x0 -> x17, Pallas kernels: none -> 6.5 us  [kernel_call(): pl.pallas_call(body, out_shape=shapes, in_specs=[near] * len(args), out_s...]
    unnamed x13 -> x10, local copies, waits for them, and re-layouts: 7.28 us -> 1.78 us
    all_to_all x1 -> x0, starting transfers between devices: 4.24 us -> none  [per_device(): lax.all_to_all(strided, 'col', split_axis=0, concat_axis=0, tiled=True)]
  transfers between devices with their start and end apart: 4 -> 24, of which waited for: 3 -> 11; matrix products, arithmetic and copies ran while one was open for 7% -> 0% of each run, Pallas kernels for 0% -> 6%
where the time goes in v1:
time: 58.9 us; the launch traced here: 58.6 us
  starting transfers between devices  33 us (56%)
  waiting for transfers between devices  16.5 us (28%)
  Pallas kernels  6.5 us (11%)
  local copies, waits for them, and re-layouts  1.78 us (3%)
  between operations  0.79 us (1%)
    ppermute x24, starting transfers between devices, send(): return lax.ppermute(value, AXES, pairs)  33 us
    ppermute x24, waiting for transfers between devices, send(): return lax.ppermute(value, AXES, pairs)  16.5 us
    pallas_call x17, Pallas kernels, kernel_call(): pl.pallas_call(body, out_shape=shapes, in_specs=[near] * len(args), out_s...  6.5 us
    unnamed x10, local copies, waits for them, and re-layouts  1.78 us
  transfers between devices with their start and end apart: 24, of which 11 were waited for; matrix products, arithmetic and copies ran while one was open for 0% of the time, Pallas kernels for 6%

profile of v1, /device:TPU:0, one launch (start us, length us, event | category | flops | bytes accessed | tf_op | source)
XLA Modules:
  0.0 58.6 jit_solution(10765510893868549983)
XLA Ops:
  0.7 1.0 %copy-done.3 = bf16[32,16,128]{2,1,0:T(8,128)(2,1)S(1)} copy-done((bf16[32,16,128]{2,1,0:T(8,128)(2,1)S(1)}, bf16[32,16,128]{2,1,0:T(8,128)(2,1)}, u32[]{:S(2)}) %copy-start.3) | copy-done | bytes 131096
  1.7 0.7 %copy-done.4 = s32[32,64]{1,0:T(8,128)S(1)} copy-done((s32[32,64]{1,0:T(8,128)S(1)}, s32[32,64]{1,0:T(8,128)}, u32[]{:S(2)}) %copy-start.4) | copy-done | bytes 8216
  3.2 0.8 %collective-permute-done.6.mate = bf16[8,32,128]{2,1,0:T(8,128)(2,1)S(1)} collective-permute-done((bf16[8,32,128]{2,1,0:T(8,128)(2,1)S(1)}, bf16[8,32,128]{2,1,0:T(8,128)(2,1)S(1)}, u32[]{:S(2)}, u32[]{:S(2)}) %collective-permute-start.6) | collective-permute-done | bytes 65568 | tf_op jit(solution)/shard_map/ppermute | solution.py:212
  4.1 3.0 %collective-permute-start.8 = (bf16[8,64,128]{2,1,0:T(8,128)(2,1)S(1)}, bf16[8,64,128]{2,1,0:T(8,128)(2,1)S(1)}, u32[]{:S(2)}, u32[]{:S(2)}) collective-permute-start(bf16[8,64,128]{2,1,0:T(8,128)(2,1)S(1)} %shard_map.72.refs_0_), channel_id=1, source_target_pairs={{0,8},{1,24},{2,0},{3,16},{4,12},{5,28},{6,4},{7,20},{8,9},{9,25},... | collective-permute-start | bytes 393224 | tf_op jit(solution)/shard_map/ppermute | solution.py:212
  7.3 0.7 %collective-permute-start.1 = (bf16[8,64,128]{2,1,0:T(8,128)(2,1)S(1)}, bf16[8,64,128]{2,1,0:T(8,128)(2,1)S(1)}, u32[]{:S(2)}, u32[]{:S(2)}) collective-permute-start(bf16[8,64,128]{2,1,0:T(8,128)(2,1)S(1)} %shard_map.69.refs_0_), channel_id=1, source_target_pairs={{0,0},{1,16},{2,8},{3,24},{4,4},{5,20},{6,12},{7,28},{8,1},{9,17},... | collective-permute-start | bytes 393224 | tf_op jit(solution)/shard_map/ppermute | solution.py:212
  7.9 0.7 %collective-permute-start.7 = (bf16[8,64,128]{2,1,0:T(8,128)(2,1)S(1)}, bf16[8,64,128]{2,1,0:T(8,128)(2,1)S(1)}, u32[]{:S(2)}, u32[]{:S(2)}) collective-permute-start(bf16[8,64,128]{2,1,0:T(8,128)(2,1)S(1)} %shard_map.72.refs_0_), channel_id=1, source_target_pairs={{0,0},{1,16},{2,8},{3,24},{4,4},{5,20},{6,12},{7,28},{8,1},{9,17},... | collective-permute-start | bytes 393224 | tf_op jit(solution)/shard_map/ppermute | solution.py:212
  8.6 8.6 %collective-permute-start.5 = (bf16[8,64,128]{2,1,0:T(8,128)(2,1)S(1)}, bf16[8,64,128]{2,1,0:T(8,128)(2,1)S(1)}, u32[]{:S(2)}, u32[]{:S(2)}) collective-permute-start(bf16[8,64,128]{2,1,0:T(8,128)(2,1)S(1)} %shard_map.69.refs_0_), channel_id=1, source_target_pairs={{0,2},{1,3},{2,0},{3,1},{4,6},{5,7},{6,4},{7,5},{8,10},{9,11},{10,... | collective-permute-start | bytes 393224 | tf_op jit(solution)/shard_map/ppermute | solution.py:212
  17.3 1.5 %collective-permute-start.4 = (bf16[8,64,128]{2,1,0:T(8,128)(2,1)S(1)}, bf16[8,64,128]{2,1,0:T(8,128)(2,1)S(1)}, u32[]{:S(2)}, u32[]{:S(2)}) collective-permute-start(bf16[8,64,128]{2,1,0:T(8,128)(2,1)S(1)} %collective-permute-done.2.refs_3_.refs_1_), channel_id=1, source_target_pairs={{0,4},{1,5},{2,6},{3,7},{4,0},{5,1},{6,2},{7,3},{8,12},{9,13},{10,... | collective-permute-start | bytes 393224 | tf_op jit(solution)/shard_map/ppermute | solution.py:212
  19.4 1.5 %collective-permute-start.10 = (bf16[8,64,128]{2,1,0:T(8,128)(2,1)S(1)}, bf16[8,64,128]{2,1,0:T(8,128)(2,1)S(1)}, u32[]{:S(2)}, u32[]{:S(2)}) collective-permute-start(bf16[8,64,128]{2,1,0:T(8,128)(2,1)S(1)} %collective-permute-done.8.refs_3_.refs_7_), channel_id=1, source_target_pairs={{0,4},{1,5},{2,6},{3,7},{4,0},{5,1},{6,2},{7,3},{8,12},{9,13},{10,... | collective-permute-start | bytes 393224 | tf_op jit(solution)/shard_map/ppermute | solution.py:212
  20.9 3.1 %collective-permute-done.5.refs_1_ = bf16[8,64,128]{2,1,0:T(8,128)(2,1)S(1)} collective-permute-done((bf16[8,64,128]{2,1,0:T(8,128)(2,1)S(1)}, bf16[8,64,128]{2,1,0:T(8,128)(2,1)S(1)}, u32[]{:S(2)}, u32[]{:S(2)}) %collective-permute-start.5) | collective-permute-done | bytes 131104 | tf_op jit(solution)/shard_map/ppermute | solution.py:212
  24.0 1.5 %collective-permute-start.9 = (bf16[8,64,128]{2,1,0:T(8,128)(2,1)S(1)}, bf16[8,64,128]{2,1,0:T(8,128)(2,1)S(1)}, u32[]{:S(2)}, u32[]{:S(2)}) collective-permute-start(bf16[8,64,128]{2,1,0:T(8,128)(2,1)S(1)} %collective-permute-done.7.refs_2_.refs_6_), channel_id=1, source_target_pairs={{0,4},{1,5},{2,6},{3,7},{4,0},{5,1},{6,2},{7,3},{8,12},{9,13},{10,... | collective-permute-start | bytes 393224 | tf_op jit(solution)/shard_map/ppermute | solution.py:212
  25.5 0.9 %shard_map.70 = (bf16[8,256,128]{2,1,0:T(8,128)(2,1)S(1)}, bf16[8,128,128]{2,1,0:T(8,128)(2,1)S(1)}) custom-call(bf16[8,64,128]{2,1,0:T(8,128)(2,1)S(1)} %shard_map.69.refs_0_, bf16[8,64,128]{2,1,0:T(8,128)(2,1)S(1)} %collective-permute-done.5.refs_1_, bf16[8,64,128]{2,1,0:T(8,128)(2,1)S(1)} %collective-permute-done.1.refs_2_.refs_0_, ...), custom_call_target="tpu_custom_call" | custom-call | flops 134217728 | bytes 4587520 | tf_op jit(solution)/shard_map/pallas_call | solution.py:45
  26.8 0.9 %shard_map.73 = (bf16[8,256,128]{2,1,0:T(8,128)(2,1)S(1)}, bf16[8,128,128]{2,1,0:T(8,128)(2,1)S(1)}) custom-call(bf16[8,64,128]{2,1,0:T(8,128)(2,1)S(1)} %shard_map.72.refs_0_, bf16[8,64,128]{2,1,0:T(8,128)(2,1)S(1)} %collective-permute-done.11.refs_1_, bf16[8,64,128]{2,1,0:T(8,128)(2,1)S(1)} %collective-permute-done.7.refs_2_.refs_6_, ...), custom_call_target="tpu_custom_call" | custom-call | flops 134217728 | bytes 4587520 | tf_op jit(solution)/shard_map/pallas_call | solution.py:45
  27.7 1.0 %shard_map.71 = (bf16[8,256,128]{2,1,0:T(8,128)(2,1)S(1)}, bf16[8,32,128]{2,1,0:T(8,128)(2,1)S(1)}, bf16[8,32,128]{2,1,0:T(8,128)(2,1)S(1)}, bf16[8,32,128]{2,1,...) custom-call(bf16[8,64,128]{2,1,0:T(8,128)(2,1)S(1)} %shard_map.69.re, ...), custom_call_target="tpu_custom_call" | custom-call | flops 134217728 | bytes 5111808 | tf_op jit(solution)/shard_map/pallas_call | solution.py:45
  28.7 2.6 %collective-permute-done.9.refs_2_.refs_8_ = bf16[8,64,128]{2,1,0:T(8,128)(2,1)S(1)} collective-permute-done((bf16[8,64,128]{2,1,0:T(8,128)(2,1)S(1)}, bf16[8,64,128]{2,1,0:T(8,128)(2,1)S(1)}, u32[]{:S(2)}, u32[]{:S(2)}) %collective-permute-start.9) | collective-permute-done | bytes 131104 | tf_op jit(solution)/shard_map/ppermute | solution.py:212
  31.2 1.0 %shard_map.74 = (bf16[8,256,128]{2,1,0:T(8,128)(2,1)S(1)}, bf16[8,32,128]{2,1,0:T(8,128)(2,1)S(1)}, bf16[8,32,128]{2,1,0:T(8,128)(2,1)S(1)}, bf16[8,32,128]{2,1,...) custom-call(bf16[8,64,128]{2,1,0:T(8,128)(2,1)S(1)} %shard_map.72.re, ...), custom_call_target="tpu_custom_call" | custom-call | flops 134217728 | bytes 5111808 | tf_op jit(solution)/shard_map/pallas_call | solution.py:45
  32.2 0.9 %shard_map.75 = (bf16[16,64,128]{2,1,0:T(8,128)(2,1)S(1)}, bf16[16,32,128]{2,1,0:T(8,128)(2,1)S(1)}, bf16[16,32,128]{2,1,0:T(8,128)(2,1)S(1)}) custom-call(bf16[8,64,128]{2,1,0:T(8,128)(2,1)S(1)} %collective-permute-done.1.refs_2_.refs_0_, bf16[8,64,128]{2,1,0:T(8,128)(2,1)S(1)} %collective-permute-done.2.refs_3_.refs_1_, ...), custom_call_target="tpu_custom_call" | custom-call | flops 268435456 | bytes 3670016 | tf_op jit(solution)/shard_map/pallas_call | solution.py:45
  33.1 0.8 %collective-permute-start.12 = (bf16[16,64,128]{2,1,0:T(8,128)(2,1)S(1)}, bf16[16,64,128]{2,1,0:T(8,128)(2,1)S(1)}, u32[]{:S(2)}, u32[]{:S(2)}) collective-permute-start(bf16[16,64,128]{2,1,0:T(8,128)(2,1)S(1)} %get-tuple-element.34), channel_id=1, source_target_pairs={{0,1},{1,0},{2,3},{3,2},{4,5},{5,4},{6,7},{7,6},{8,9},{9,8},{10,11... | collective-permute-start | bytes 786440 | tf_op jit(solution)/shard_map/ppermute | solution.py:212
  33.9 1.5 %collective-permute-start.14 = (bf16[8,64,128]{2,1,0:T(8,128)(2,1)S(1)}, bf16[8,64,128]{2,1,0:T(8,128)(2,1)S(1)}, u32[]{:S(2)}, u32[]{:S(2)}) collective-permute-start(bf16[8,64,128]{2,1,0:T(8,128)(2,1)S(1)} %get-tuple-element.37), channel_id=1, source_target_pairs={{0,4},{1,5},{2,6},{3,7},{4,0},{5,1},{6,2},{7,3},{8,12},{9,13},{10,... | collective-permute-start | bytes 393224 | tf_op jit(solution)/shard_map/ppermute | solution.py:212
  35.9 1.5 %collective-permute-start.19 = (bf16[8,64,128]{2,1,0:T(8,128)(2,1)S(1)}, bf16[8,64,128]{2,1,0:T(8,128)(2,1)S(1)}, u32[]{:S(2)}, u32[]{:S(2)}) collective-permute-start(bf16[8,64,128]{2,1,0:T(8,128)(2,1)S(1)} %get-tuple-element.43), channel_id=1, source_target_pairs={{0,4},{1,5},{2,6},{3,7},{4,0},{5,1},{6,2},{7,3},{8,12},{9,13},{10,... | collective-permute-start | bytes 393224 | tf_op jit(solution)/shard_map/ppermute | solution.py:212
  38.0 2.3 %collective-permute-done.14.refs_1_ = bf16[8,64,128]{2,1,0:T(8,128)(2,1)S(1)} collective-permute-done((bf16[8,64,128]{2,1,0:T(8,128)(2,1)S(1)}, bf16[8,64,128]{2,1,0:T(8,128)(2,1)S(1)}, u32[]{:S(2)}, u32[]{:S(2)}) %collective-permute-start.14) | collective-permute-done | bytes 131104 | tf_op jit(solution)/shard_map/ppermute | solution.py:212
  40.7 2.4 %collective-permute-done.16.refs_1_ = bf16[8,64,128]{2,1,0:T(8,128)(2,1)S(1)} collective-permute-done((bf16[8,64,128]{2,1,0:T(8,128)(2,1)S(1)}, bf16[8,64,128]{2,1,0:T(8,128)(2,1)S(1)}, u32[]{:S(2)}, u32[]{:S(2)}) %collective-permute-start.16) | collective-permute-done | bytes 131104 | tf_op jit(solution)/shard_map/ppermute | solution.py:212
  43.1 1.4 %collective-permute-start.17 = (bf16[8,32,128]{2,1,0:T(8,128)(2,1)S(1)}, bf16[8,32,128]{2,1,0:T(8,128)(2,1)S(1)}, u32[]{:S(2)}, u32[]{:S(2)}) collective-permute-start(bf16[8,32,128]{2,1,0:T(8,128)(2,1)S(1)} %shard_map.79), channel_id=1, source_target_pairs={{0,16},{1,17},{2,18},{3,19},{4,20},{5,21},{6,22},{7,23},{8,24},{9,... | collective-permute-start | bytes 196616 | tf_op jit(solution)/shard_map/ppermute | solution.py:212
  44.5 1.2 %collective-permute-start.13 = (bf16[16,32,128]{2,1,0:T(8,128)(2,1)S(1)}, bf16[16,32,128]{2,1,0:T(8,128)(2,1)S(1)}, u32[]{:S(2)}, u32[]{:S(2)}) collective-permute-start(bf16[16,32,128]{2,1,0:T(8,128)(2,1)S(1)} %shard_map.76), channel_id=1, source_target_pairs={{0,2},{1,3},{2,0},{3,1},{4,6},{5,7},{6,4},{7,5},{8,10},{9,11},{10,... | collective-permute-start | bytes 393224 | tf_op jit(solution)/shard_map/ppermute | solution.py:212
  45.9 1.8 %collective-permute-start.18 = (bf16[8,32,128]{2,1,0:T(8,128)(2,1)S(1)}, bf16[8,32,128]{2,1,0:T(8,128)(2,1)S(1)}, u32[]{:S(2)}, u32[]{:S(2)}) collective-permute-start(bf16[8,32,128]{2,1,0:T(8,128)(2,1)S(1)} %shard_map.80), channel_id=1, source_target_pairs={{0,24},{1,25},{2,26},{3,27},{4,28},{5,29},{6,30},{7,31},{8,16},{9,... | collective-permute-start | bytes 196616 | tf_op jit(solution)/shard_map/ppermute | solution.py:212
  47.8 1.1 %collective-permute-start.20 = (bf16[8,32,128]{2,1,0:T(8,128)(2,1)S(1)}, bf16[8,32,128]{2,1,0:T(8,128)(2,1)S(1)}, u32[]{:S(2)}, u32[]{:S(2)}) collective-permute-start(bf16[8,32,128]{2,1,0:T(8,128)(2,1)S(1)} %shard_map.81), channel_id=1, source_target_pairs={{0,8},{1,9},{2,10},{3,11},{4,12},{5,13},{6,14},{7,15},{8,0},{9,1},... | collective-permute-start | bytes 196616 | tf_op jit(solution)/shard_map/ppermute | solution.py:212
  49.0 1.7 %collective-permute-start.22 = (bf16[8,32,128]{2,1,0:T(8,128)(2,1)S(1)}, bf16[8,32,128]{2,1,0:T(8,128)(2,1)S(1)}, u32[]{:S(2)}, u32[]{:S(2)}) collective-permute-start(bf16[8,32,128]{2,1,0:T(8,128)(2,1)S(1)} %shard_map.82), channel_id=1, source_target_pairs={{0,16},{1,17},{2,18},{3,19},{4,20},{5,21},{6,22},{7,23},{8,24},{9,... | collective-permute-start | bytes 196616 | tf_op jit(solution)/shard_map/ppermute | solution.py:212
  50.7 1.7 %collective-permute-start.23 = (bf16[8,32,128]{2,1,0:T(8,128)(2,1)S(1)}, bf16[8,32,128]{2,1,0:T(8,128)(2,1)S(1)}, u32[]{:S(2)}, u32[]{:S(2)}) collective-permute-start(bf16[8,32,128]{2,1,0:T(8,128)(2,1)S(1)} %shard_map.83), channel_id=1, source_target_pairs={{0,24},{1,25},{2,26},{3,27},{4,28},{5,29},{6,30},{7,31},{8,16},{9,... | collective-permute-start | bytes 196616 | tf_op jit(solution)/shard_map/ppermute | solution.py:212
  52.8 0.6 %collective-permute-done.20.refs_7_ = bf16[8,32,128]{2,1,0:T(8,128)(2,1)S(1)} collective-permute-done((bf16[8,32,128]{2,1,0:T(8,128)(2,1)S(1)}, bf16[8,32,128]{2,1,0:T(8,128)(2,1)S(1)}, u32[]{:S(2)}, u32[]{:S(2)}) %collective-permute-start.20) | collective-permute-done | bytes 65568 | tf_op jit(solution)/shard_map/ppermute | solution.py:212
  53.4 3.6 %collective-permute-done.22.refs_8_ = bf16[8,32,128]{2,1,0:T(8,128)(2,1)S(1)} collective-permute-done((bf16[8,32,128]{2,1,0:T(8,128)(2,1)S(1)}, bf16[8,32,128]{2,1,0:T(8,128)(2,1)S(1)}, u32[]{:S(2)}, u32[]{:S(2)}) %collective-permute-start.22) | collective-permute-done | bytes 65568 | tf_op jit(solution)/shard_map/ppermute | solution.py:212
  57.0 0.8 %shard_map.84 = bf16[32,16,128]{2,1,0:T(8,128)(2,1)} custom-call(bf16[8,32,128]{2,1,0:T(8,128)(2,1)S(1)} %get-tuple-element.36.refs_0_, bf16[8,64,128]{2,1,0:T(8,128)(2,1)S(1)} %collective-permute-done.14.refs_1_, bf16[8,32,128]{2,1,0:T(8,128)(2,1)S(1)} %collective-permute-done.15.refs_2_, bf16[8,32,128]{2,1,0:T(8,128)(2,1)S(1)} %collective-permute-done.17.refs_3_, ...), custom_call_target="tpu_custom_call" | custom-call | flops 262144 | bytes 917504 | tf_op jit(solution)/shard_map/pallas_call | solution.py:45
  57.8 0.8 %shard_map.77 = bf16[32,16,128]{2,1,0:T(8,128)(2,1)} custom-call(bf16[16,32,128]{2,1,0:T(8,128)(2,1)S(1)} %get-tuple-element.33.refs_0_, bf16[16,64,128]{2,1,0:T(8,128)(2,1)S(1)} %collective-permute-done.12.refs_1_, bf16[16,32,128]{2,1,0:T(8,128)(2,1)S(1)} %collective-permute-done.13.refs_2_), custom_call_target="tpu_custom_call" | custom-call | flops 262144 | bytes 655360 | tf_op jit(solution)/shard_map/pallas_call | solution.py:45
  (43 shorter events, 4.4 us)
Async XLA Ops:
  0.6 24.9 %copy-start = (bf16[2,16,128,256]{3,2,1,0:T(8,128)(2,1)S(1)}, bf16[2,16,128,256]{3,2,1,0:T(8,128)(2,1)}, u32[]{:S(2)}) copy-start(bf16[2,16,128,256]{3,2,1,0:T(8,128)(2,1)} %refs_6_.7) | copy-start | bytes 6291460
  0.6 24.9 %copy-start.1 = (bf16[16,128,256]{2,1,0:T(8,128)(2,1)S(1)}, bf16[16,128,256]{2,1,0:T(8,128)(2,1)}, u32[]{:S(2)}) copy-start(bf16[16,128,256]{2,1,0:T(8,128)(2,1)} %refs_5_.7) | copy-start | bytes 3145732
  0.7 1.1 %copy-start.3 = (bf16[32,16,128]{2,1,0:T(8,128)(2,1)S(1)}, bf16[32,16,128]{2,1,0:T(8,128)(2,1)}, u32[]{:S(2)}) copy-start(bf16[32,16,128]{2,1,0:T(8,128)(2,1)} %spectra.1) | copy-start | bytes 393220
  1.7 0.7 %copy-start.4 = (s32[32,64]{1,0:T(8,128)S(1)}, s32[32,64]{1,0:T(8,128)}, u32[]{:S(2)}) copy-start(s32[32,64]{1,0:T(8,128)} %flags.1) | copy-start | bytes 24580
  2.4 23.1 %copy-start.2 = (s32[128,256]{1,0:T(8,128)S(1)}, s32[128,256]{1,0:T(8,128)}, u32[]{:S(2)}) copy-start(s32[128,256]{1,0:T(8,128)} %refs_4_.7) | copy-start | bytes 393220
  2.6 1.5 %collective-permute-start.6 = (bf16[8,32,128]{2,1,0:T(8,128)(2,1)S(1)}, bf16[8,32,128]{2,1,0:T(8,128)(2,1)S(1)}, u32[]{:S(2)}, u32[]{:S(2)}) collective-permute-start(bf16[8,32,128]{2,1,0:T(8,128)(2,1)S(1)} %get-tuple-element.29.own), channel_id=1, source_target_pairs={{0,1},{1,0},{2,3},{3,2},{4,5},{5,4},{6,7},{7,6},{8,9},{9,8},{10,11... | collective-permute-start | bytes 196616 | tf_op jit(solution)/shard_map/ppermute | solution.py:212
  3.1 3.9 %collective-permute-start = (bf16[8,32,128]{2,1,0:T(8,128)(2,1)S(1)}, bf16[8,32,128]{2,1,0:T(8,128)(2,1)S(1)}, u32[]{:S(2)}, u32[]{:S(2)}) collective-permute-start(bf16[8,32,128]{2,1,0:T(8,128)(2,1)S(1)} %get-tuple-element.25.own), channel_id=1, source_target_pairs={{0,1},{1,0},{2,3},{3,2},{4,5},{5,4},{6,7},{7,6},{8,9},{9,8},{10,11... | collective-permute-start | bytes 196616 | tf_op jit(solution)/shard_map/ppermute | solution.py:212
  4.1 13.2 %collective-permute-start.8 = (bf16[8,64,128]{2,1,0:T(8,128)(2,1)S(1)}, bf16[8,64,128]{2,1,0:T(8,128)(2,1)S(1)}, u32[]{:S(2)}, u32[]{:S(2)}) collective-permute-start(bf16[8,64,128]{2,1,0:T(8,128)(2,1)S(1)} %shard_map.72.refs_0_), channel_id=1, source_target_pairs={{0,8},{1,24},{2,0},{3,16},{4,12},{5,28},{6,4},{7,20},{8,9},{9,25},... | collective-permute-start | bytes 393224 | tf_op jit(solution)/shard_map/ppermute | solution.py:212
  7.1 10.3 %collective-permute-start.2 = (bf16[8,64,128]{2,1,0:T(8,128)(2,1)S(1)}, bf16[8,64,128]{2,1,0:T(8,128)(2,1)S(1)}, u32[]{:S(2)}, u32[]{:S(2)}) collective-permute-start(bf16[8,64,128]{2,1,0:T(8,128)(2,1)S(1)} %shard_map.69.refs_0_), channel_id=1, source_target_pairs={{0,8},{1,24},{2,0},{3,16},{4,12},{5,28},{6,4},{7,20},{8,9},{9,25},... | collective-permute-start | bytes 393224 | tf_op jit(solution)/shard_map/ppermute | solution.py:212
  7.3 11.6 %collective-permute-start.1 = (bf16[8,64,128]{2,1,0:T(8,128)(2,1)S(1)}, bf16[8,64,128]{2,1,0:T(8,128)(2,1)S(1)}, u32[]{:S(2)}, u32[]{:S(2)}) collective-permute-start(bf16[8,64,128]{2,1,0:T(8,128)(2,1)S(1)} %shard_map.69.refs_0_), channel_id=1, source_target_pairs={{0,0},{1,16},{2,8},{3,24},{4,4},{5,20},{6,12},{7,28},{8,1},{9,17},... | collective-permute-start | bytes 393224 | tf_op jit(solution)/shard_map/ppermute | solution.py:212
  7.9 11.5 %collective-permute-start.7 = (bf16[8,64,128]{2,1,0:T(8,128)(2,1)S(1)}, bf16[8,64,128]{2,1,0:T(8,128)(2,1)S(1)}, u32[]{:S(2)}, u32[]{:S(2)}) collective-permute-start(bf16[8,64,128]{2,1,0:T(8,128)(2,1)S(1)} %shard_map.72.refs_0_), channel_id=1, source_target_pairs={{0,0},{1,16},{2,8},{3,24},{4,4},{5,20},{6,12},{7,28},{8,1},{9,17},... | collective-permute-start | bytes 393224 | tf_op jit(solution)/shard_map/ppermute | solution.py:212
  8.6 15.4 %collective-permute-start.5 = (bf16[8,64,128]{2,1,0:T(8,128)(2,1)S(1)}, bf16[8,64,128]{2,1,0:T(8,128)(2,1)S(1)}, u32[]{:S(2)}, u32[]{:S(2)}) collective-permute-start(bf16[8,64,128]{2,1,0:T(8,128)(2,1)S(1)} %shard_map.69.refs_0_), channel_id=1, source_target_pairs={{0,2},{1,3},{2,0},{3,1},{4,6},{5,7},{6,4},{7,5},{8,10},{9,11},{10,... | collective-permute-start | bytes 393224 | tf_op jit(solution)/shard_map/ppermute | solution.py:212
  17.3 9.5 %collective-permute-start.11 = (bf16[8,64,128]{2,1,0:T(8,128)(2,1)S(1)}, bf16[8,64,128]{2,1,0:T(8,128)(2,1)S(1)}, u32[]{:S(2)}, u32[]{:S(2)}) collective-permute-start(bf16[8,64,128]{2,1,0:T(8,128)(2,1)S(1)} %shard_map.72.refs_0_), channel_id=1, source_target_pairs={{0,2},{1,3},{2,0},{3,1},{4,6},{5,7},{6,4},{7,5},{8,10},{9,11},{10,... | collective-permute-start | bytes 393224 | tf_op jit(solution)/shard_map/ppermute | solution.py:212
  17.3 10.3 %collective-permute-start.4 = (bf16[8,64,128]{2,1,0:T(8,128)(2,1)S(1)}, bf16[8,64,128]{2,1,0:T(8,128)(2,1)S(1)}, u32[]{:S(2)}, u32[]{:S(2)}) collective-permute-start(bf16[8,64,128]{2,1,0:T(8,128)(2,1)S(1)} %collective-permute-done.2.refs_3_.refs_1_), channel_id=1, source_target_pairs={{0,4},{1,5},{2,6},{3,7},{4,0},{5,1},{6,2},{7,3},{8,12},{9,13},{10,... | collective-permute-start | bytes 393224 | tf_op jit(solution)/shard_map/ppermute | solution.py:212
  18.9 8.8 %collective-permute-start.3 = (bf16[8,64,128]{2,1,0:T(8,128)(2,1)S(1)}, bf16[8,64,128]{2,1,0:T(8,128)(2,1)S(1)}, u32[]{:S(2)}, u32[]{:S(2)}) collective-permute-start(bf16[8,64,128]{2,1,0:T(8,128)(2,1)S(1)} %collective-permute-done.1.refs_2_.refs_0_), channel_id=1, source_target_pairs={{0,4},{1,5},{2,6},{3,7},{4,0},{5,1},{6,2},{7,3},{8,12},{9,13},{10,... | collective-permute-start | bytes 393224 | tf_op jit(solution)/shard_map/ppermute | solution.py:212
  19.4 9.3 %collective-permute-start.10 = (bf16[8,64,128]{2,1,0:T(8,128)(2,1)S(1)}, bf16[8,64,128]{2,1,0:T(8,128)(2,1)S(1)}, u32[]{:S(2)}, u32[]{:S(2)}) collective-permute-start(bf16[8,64,128]{2,1,0:T(8,128)(2,1)S(1)} %collective-permute-done.8.refs_3_.refs_7_), channel_id=1, source_target_pairs={{0,4},{1,5},{2,6},{3,7},{4,0},{5,1},{6,2},{7,3},{8,12},{9,13},{10,... | collective-permute-start | bytes 393224 | tf_op jit(solution)/shard_map/ppermute | solution.py:212
  24.0 7.3 %collective-permute-start.9 = (bf16[8,64,128]{2,1,0:T(8,128)(2,1)S(1)}, bf16[8,64,128]{2,1,0:T(8,128)(2,1)S(1)}, u32[]{:S(2)}, u32[]{:S(2)}) collective-permute-start(bf16[8,64,128]{2,1,0:T(8,128)(2,1)S(1)} %collective-permute-done.7.refs_2_.refs_6_), channel_id=1, source_target_pairs={{0,4},{1,5},{2,6},{3,7},{4,0},{5,1},{6,2},{7,3},{8,12},{9,13},{10,... | collective-permute-start | bytes 393224 | tf_op jit(solution)/shard_map/ppermute | solution.py:212
  33.1 11.4 %collective-permute-start.12 = (bf16[16,64,128]{2,1,0:T(8,128)(2,1)S(1)}, bf16[16,64,128]{2,1,0:T(8,128)(2,1)S(1)}, u32[]{:S(2)}, u32[]{:S(2)}) collective-permute-start(bf16[16,64,128]{2,1,0:T(8,128)(2,1)S(1)} %get-tuple-element.34), channel_id=1, source_target_pairs={{0,1},{1,0},{2,3},{3,2},{4,5},{5,4},{6,7},{7,6},{8,9},{9,8},{10,11... | collective-permute-start | bytes 786440 | tf_op jit(solution)/shard_map/ppermute | solution.py:212
  33.9 6.4 %collective-permute-start.14 = (bf16[8,64,128]{2,1,0:T(8,128)(2,1)S(1)}, bf16[8,64,128]{2,1,0:T(8,128)(2,1)S(1)}, u32[]{:S(2)}, u32[]{:S(2)}) collective-permute-start(bf16[8,64,128]{2,1,0:T(8,128)(2,1)S(1)} %get-tuple-element.37), channel_id=1, source_target_pairs={{0,4},{1,5},{2,6},{3,7},{4,0},{5,1},{6,2},{7,3},{8,12},{9,13},{10,... | collective-permute-start | bytes 393224 | tf_op jit(solution)/shard_map/ppermute | solution.py:212
  35.4 7.7 %collective-permute-start.16 = (bf16[8,64,128]{2,1,0:T(8,128)(2,1)S(1)}, bf16[8,64,128]{2,1,0:T(8,128)(2,1)S(1)}, u32[]{:S(2)}, u32[]{:S(2)}) collective-permute-start(bf16[8,64,128]{2,1,0:T(8,128)(2,1)S(1)} %get-tuple-element.40), channel_id=1, source_target_pairs={{0,4},{1,5},{2,6},{3,7},{4,0},{5,1},{6,2},{7,3},{8,12},{9,13},{10,... | collective-permute-start | bytes 393224 | tf_op jit(solution)/shard_map/ppermute | solution.py:212
  35.9 10.0 %collective-permute-start.19 = (bf16[8,64,128]{2,1,0:T(8,128)(2,1)S(1)}, bf16[8,64,128]{2,1,0:T(8,128)(2,1)S(1)}, u32[]{:S(2)}, u32[]{:S(2)}) collective-permute-start(bf16[8,64,128]{2,1,0:T(8,128)(2,1)S(1)} %get-tuple-element.43), channel_id=1, source_target_pairs={{0,4},{1,5},{2,6},{3,7},{4,0},{5,1},{6,2},{7,3},{8,12},{9,13},{10,... | collective-permute-start | bytes 393224 | tf_op jit(solution)/shard_map/ppermute | solution.py:212
  37.5 10.4 %collective-permute-start.21 = (bf16[8,64,128]{2,1,0:T(8,128)(2,1)S(1)}, bf16[8,64,128]{2,1,0:T(8,128)(2,1)S(1)}, u32[]{:S(2)}, u32[]{:S(2)}) collective-permute-start(bf16[8,64,128]{2,1,0:T(8,128)(2,1)S(1)} %get-tuple-element.46), channel_id=1, source_target_pairs={{0,4},{1,5},{2,6},{3,7},{4,0},{5,1},{6,2},{7,3},{8,12},{9,13},{10,... | collective-permute-start | bytes 393224 | tf_op jit(solution)/shard_map/ppermute | solution.py:212
  40.3 8.7 %collective-permute-start.15 = (bf16[8,32,128]{2,1,0:T(8,128)(2,1)S(1)}, bf16[8,32,128]{2,1,0:T(8,128)(2,1)S(1)}, u32[]{:S(2)}, u32[]{:S(2)}) collective-permute-start(bf16[8,32,128]{2,1,0:T(8,128)(2,1)S(1)} %shard_map.78), channel_id=1, source_target_pairs={{0,8},{1,9},{2,10},{3,11},{4,12},{5,13},{6,14},{7,15},{8,0},{9,1},... | collective-permute-start | bytes 196616 | tf_op jit(solution)/shard_map/ppermute | solution.py:212
  43.1 7.6 %collective-permute-start.17 = (bf16[8,32,128]{2,1,0:T(8,128)(2,1)S(1)}, bf16[8,32,128]{2,1,0:T(8,128)(2,1)S(1)}, u32[]{:S(2)}, u32[]{:S(2)}) collective-permute-start(bf16[8,32,128]{2,1,0:T(8,128)(2,1)S(1)} %shard_map.79), channel_id=1, source_target_pairs={{0,16},{1,17},{2,18},{3,19},{4,20},{5,21},{6,22},{7,23},{8,24},{9,... | collective-permute-start | bytes 196616 | tf_op jit(solution)/shard_map/ppermute | solution.py:212
  44.5 13.3 %collective-permute-start.13 = (bf16[16,32,128]{2,1,0:T(8,128)(2,1)S(1)}, bf16[16,32,128]{2,1,0:T(8,128)(2,1)S(1)}, u32[]{:S(2)}, u32[]{:S(2)}) collective-permute-start(bf16[16,32,128]{2,1,0:T(8,128)(2,1)S(1)} %shard_map.76), channel_id=1, source_target_pairs={{0,2},{1,3},{2,0},{3,1},{4,6},{5,7},{6,4},{7,5},{8,10},{9,11},{10,... | collective-permute-start | bytes 393224 | tf_op jit(solution)/shard_map/ppermute | solution.py:212
  45.9 6.9 %collective-permute-start.18 = (bf16[8,32,128]{2,1,0:T(8,128)(2,1)S(1)}, bf16[8,32,128]{2,1,0:T(8,128)(2,1)S(1)}, u32[]{:S(2)}, u32[]{:S(2)}) collective-permute-start(bf16[8,32,128]{2,1,0:T(8,128)(2,1)S(1)} %shard_map.80), channel_id=1, source_target_pairs={{0,24},{1,25},{2,26},{3,27},{4,28},{5,29},{6,30},{7,31},{8,16},{9,... | collective-permute-start | bytes 196616 | tf_op jit(solution)/shard_map/ppermute | solution.py:212
  47.8 5.6 %collective-permute-start.20 = (bf16[8,32,128]{2,1,0:T(8,128)(2,1)S(1)}, bf16[8,32,128]{2,1,0:T(8,128)(2,1)S(1)}, u32[]{:S(2)}, u32[]{:S(2)}) collective-permute-start(bf16[8,32,128]{2,1,0:T(8,128)(2,1)S(1)} %shard_map.81), channel_id=1, source_target_pairs={{0,8},{1,9},{2,10},{3,11},{4,12},{5,13},{6,14},{7,15},{8,0},{9,1},... | collective-permute-start | bytes 196616 | tf_op jit(solution)/shard_map/ppermute | solution.py:212
  49.0 8.0 %collective-permute-start.22 = (bf16[8,32,128]{2,1,0:T(8,128)(2,1)S(1)}, bf16[8,32,128]{2,1,0:T(8,128)(2,1)S(1)}, u32[]{:S(2)}, u32[]{:S(2)}) collective-permute-start(bf16[8,32,128]{2,1,0:T(8,128)(2,1)S(1)} %shard_map.82), channel_id=1, source_target_pairs={{0,16},{1,17},{2,18},{3,19},{4,20},{5,21},{6,22},{7,23},{8,24},{9,... | collective-permute-start | bytes 196616 | tf_op jit(solution)/shard_map/ppermute | solution.py:212
  50.7 6.3 %collective-permute-start.23 = (bf16[8,32,128]{2,1,0:T(8,128)(2,1)S(1)}, bf16[8,32,128]{2,1,0:T(8,128)(2,1)S(1)}, u32[]{:S(2)}, u32[]{:S(2)}) collective-permute-start(bf16[8,32,128]{2,1,0:T(8,128)(2,1)S(1)} %shard_map.83), channel_id=1, source_target_pairs={{0,24},{1,25},{2,26},{3,27},{4,28},{5,29},{6,30},{7,31},{8,16},{9,... | collective-permute-start | bytes 196616 | tf_op jit(solution)/shard_map/ppermute | solution.py:212
